TPU v7x, 512 devices: a whole 4x4x16 slice. The times are simulated.
512 devices in a mesh: dp: 64 (over z, y), tensor: 8 (over x, core).
Axes of the slice: x: 4, y: 4, z: 16, core: 2. Of those that a mesh axis runs over, the one named last changes fastest.
Arguments:
- layer_input: bfloat16 [8192, 8192], P('dp', 'tensor'), may hold values from -6 to 6
- output_grad: bfloat16 [8192, 8192], P('dp', 'tensor'), may hold values from -0.06591797 to 0.06591797
- gate_pre: bfloat16 [8192, 28672], P('dp', 'tensor'), may hold values from -6 to 6
- up_pre: bfloat16 [8192, 28672], P('dp', 'tensor'), may hold values from -6 to 6
- hidden_grad: bfloat16 [8192, 28672], P('dp', 'tensor'), may hold values from -0.06591797 to 0.06591797
- tile_list: int32 [448, 3], P('tensor'), may hold values from 0 to 63, as said below
- tile_slots: int32 [448], P('tensor'), may hold values from 0 to 127, as said below
- first_codes: int32 [8, 128, 16384], P('tensor', 'dp'), may hold values from 0 to 255
- second_codes: int32 [8, 128, 16384], P('tensor', 'dp'), may hold values from 0 to 255
- first_absmax: float32 [8, 128, 8], P('tensor', 'dp'), may hold values from 0.05 to 0.5
- second_absmax: float32 [8, 128, 8], P('tensor', 'dp'), may hold values from 0.005 to 0.05
- signed_map: float32 [256], replicated, may hold values from -1 to 1
- unsigned_map: float32 [256], replicated, may hold values from 0.05 to 1
Outputs:
- update_tiles: bfloat16 [448, 128, 128], P('tensor')
- first_moment: float32 [8, 128, 16384], P('tensor', 'dp')
- second_moment: float32 [8, 128, 16384], P('tensor', 'dp')
Inputs may be any that keep to these rules, and one draw needn't show every extreme that they name: `tile_list`: within each group of 56 rows that belongs to one tensor index the triples are distinct; the first entry is below 64, the second below 28, the third is 0, 1 or 2. `tile_slots`: within each group of 56 entries the slots are distinct; a dp index owns slots s with s // 2 equal to it, so it holds at most 2 tiles of a group, and in every group some dp index holds exactly 2.
All inputs are finite; a program needn't handle non-finite values.
Results may differ from a plain program's by a relative error of at most 0.0085.
Values may be sent and summed in bfloat16 or wider, within the bound.
A program may use at most 64 MiB of HBM per device.

v0:
```python
import jax
import jax.numpy as jnp
from jax import lax
from jax.sharding import PartitionSpec as P

CAP = 2
TB = 128
STEP = 10
BETA_FIRST = 0.9
BETA_SECOND = 0.99
EPSILON = 1e-08


def lookup(code_table, level_table):
    levels = jnp.arange(16, dtype=jnp.int32)
    high_part = jnp.right_shift(code_table, 4)
    low_part = jnp.bitwise_and(code_table, 15)
    low_onehot = (low_part[:, None, :] == levels[None, :, None]).astype(jnp.bfloat16)
    high_onehot = (high_part[:, None, :] == levels[None, :, None]).astype(jnp.float32)
    square = level_table.reshape(16, 16)
    first_part = square.astype(jnp.bfloat16)
    remain = square - first_part.astype(jnp.float32)
    second_part = remain.astype(jnp.bfloat16)
    third_part = (remain - second_part.astype(jnp.float32)).astype(jnp.bfloat16)
    total = jnp.zeros(code_table.shape, jnp.float32)
    for level_part in (third_part, second_part, first_part):
        by_high = jnp.einsum(
            "hl,cln->chn", level_part, low_onehot, preferred_element_type=jnp.float32
        )
        total = total + jnp.sum(by_high * high_onehot, axis=1)
    return total


def dequantize(code_table, level_table, scales):
    values = lookup(code_table, level_table)
    shaped = values.reshape(code_table.shape[0], scales.shape[1], -1) * scales[:, :, None]
    return shaped.reshape(code_table.shape)


def body(
    layer_input,
    output_grad,
    gate_pre,
    up_pre,
    hidden_grad,
    tile_list,
    tile_slots,
    first_codes,
    second_codes,
    first_absmax,
    second_absmax,
    signed_map,
    unsigned_map,
):
    whole_input, whole_grad = (
        lax.all_gather(layer_input, "tensor", axis=1, tiled=True),
        lax.all_gather(output_grad, "tensor", axis=1, tiled=True),
    )
    tokens_here = whole_input.shape[0]
    tile_count = tile_list.shape[0]
    gate_value = gate_pre.astype(jnp.float32)
    up_value = up_pre.astype(jnp.float32)
    grad_value = hidden_grad.astype(jnp.float32)
    sigmoid_gate = jax.nn.sigmoid(gate_value)
    silu_gate = gate_value * sigmoid_gate
    hidden = (silu_gate * up_value).astype(jnp.bfloat16)
    gate_grad = (
        grad_value * up_value * sigmoid_gate * (1.0 + gate_value * (1.0 - sigmoid_gate))
    ).astype(jnp.bfloat16)
    up_grad = (grad_value * silu_gate).astype(jnp.bfloat16)
    width_block = tile_list[:, 0]
    hidden_block = tile_list[:, 1]
    matrix_id = tile_list[:, 2][None, :, None]

    def blocks(source, block_index):
        return jnp.take(source.reshape(tokens_here, -1, TB), block_index, axis=1)

    left_side = jnp.where(
        matrix_id == 2, blocks(hidden, hidden_block), blocks(whole_input, width_block)
    )
    right_side = jnp.where(
        matrix_id == 0,
        blocks(gate_grad, hidden_block),
        jnp.where(matrix_id == 1, blocks(up_grad, hidden_block), blocks(whole_grad, width_block)),
    )
    partial_value = jnp.einsum(
        "tki,tkj->kij", left_side, right_side, preferred_element_type=jnp.float32
    )
    partial_value = partial_value.reshape(tile_count, -1)
    owner_index = lax.axis_index("dp")
    slot_ids = owner_index * CAP + jnp.arange(CAP, dtype=jnp.int32)
    summed = lax.psum(partial_value, "dp")
    slot_match = (tile_slots[None, :] == slot_ids[:, None]).astype(jnp.float32)
    own_grad = jnp.dot(slot_match, summed, precision=lax.Precision.HIGHEST)
    first_old = dequantize(first_codes[0], signed_map, first_absmax[0])
    second_old = dequantize(second_codes[0], unsigned_map, second_absmax[0])
    first_moment = BETA_FIRST * first_old + (1.0 - BETA_FIRST) * own_grad
    second_moment = BETA_SECOND * second_old + (1.0 - BETA_SECOND) * own_grad * own_grad
    first_hat = first_moment / (1.0 - BETA_FIRST**STEP)
    second_hat = second_moment / (1.0 - BETA_SECOND**STEP)
    slot_update = (first_hat / (jnp.sqrt(second_hat) + EPSILON)).astype(jnp.bfloat16)
    everyone = lax.all_gather(slot_update, "dp", axis=0, tiled=True)
    picked = jnp.take(everyone, tile_slots, axis=0)
    return (picked.reshape(tile_count, TB, TB), first_moment[None], second_moment[None])


def solution(mesh):
    in_specs = (
        P("dp", "tensor"),
        P("dp", "tensor"),
        P("dp", "tensor"),
        P("dp", "tensor"),
        P("dp", "tensor"),
        P("tensor", None),
        P("tensor"),
        P("tensor", "dp", None),
        P("tensor", "dp", None),
        P("tensor", "dp", None),
        P("tensor", "dp", None),
        P(),
        P(),
    )
    out_specs = (P("tensor", None, None), P("tensor", "dp", None), P("tensor", "dp", None))
    return jax.shard_map(body, mesh=mesh, in_specs=in_specs, out_specs=out_specs, check_vma=False)
```

profile of v0, /device:TPU:2, one launch (start us, length us, event | category | flops | bytes accessed | tf_op | source)
XLA Modules:
  0.0 557.6 jit_solution(2680922352320135020)
XLA Ops:
  7.2 1.9 copy.42
  9.2 1.8 copy.37
  12.5 1.3 copy.35
  13.8 1.3 copy.39
  15.1 3.5 fusion.6
  19.2 1.6 copy.40
  20.8 2.2 gather_fusion.1
  23.0 2.0 gather_fusion.3
  25.7 2.1 gather_fusion.4
  30.0 16.4 %all-gather.7.cloned.1.call-done = bf16[128,8192]{0,1:T(8,128)(2,1)} async-done(((bf16[128,1024]{0,1:T(8,128)(2,1)}), bf16[128,8192]{0,1:T(8,128)(2,1)}) %all-gather.7.cloned.1.call-update) | async-done | bytes 2097168 | tf_op jit(solution)/shard_map/all_gather | solution.py:57
  46.4 3.2 copy.43
  49.7 32.4 %all-gather.5.cloned.1.call-done = bf16[128,8192]{0,1:T(8,128)(2,1)} async-done(((bf16[128,1024]{0,1:T(8,128)(2,1)}), bf16[128,8192]{0,1:T(8,128)(2,1)}) %all-gather.5.cloned.1.call-update) | async-done | bytes 2097168 | tf_op jit(solution)/shard_map/all_gather | solution.py:56
  82.0 4.1 copy.38
  86.1 2.0 gather_fusion.5
  88.1 3.8 gather_fusion.2
  91.9 4.2 fusion.16
  96.1 3.9 copy.51
  103.7 0.9 fusion.31
  105.5 284.1 %all-reduce.2.cloned.1.call-done = f32[56,16384]{1,0:T(8,128)} async-done(((f32[56,16384]{1,0:T(8,128)}), f32[56,16384]{1,0:T(8,128)}) %all-reduce.2.cloned.1.call-update) | async-done | bytes 3670032 | tf_op jit(solution)/shard_map/psum | solution.py:92
  389.6 4.4 fusion.46
  394.1 141.6 %all-gather.9.cloned.1.call-done = bf16[64,2,16384]{2,1,0:T(2,128)(2,1)} async-done(((bf16[1,2,16384]{2,1,0:T(2,128)(2,1)}), bf16[64,2,16384]{2,1,0:T(2,128)(2,1)}) %all-gather.9.cloned.1.call-update) | async-done | bytes 4194320 | tf_op jit(solution)/shard_map/all_gather | solution.py:102
  535.7 7.2 %reshape.189 = bf16[128,16384]{1,0:T(8,128)(2,1)} reshape(bf16[64,2,16384]{2,1,0:T(2,128)(2,1)} %all-gather.9.cloned.1.call-done) | data formatting | bytes 8388608
  543.0 6.0 %gather_fusion = bf16[56,16384]{1,0:T(8,128)(2,1)S(1)} fusion(bf16[128,16384]{1,0:T(8,128)(2,1)} %reshape.189, s32[1024]{0:T(1024)S(1)} %pad_clamp_fusion), kind=kCustom, calls=%fused_computation.5 | custom fusion | bytes 3670240 | tf_op jit(solution)/shard_map/jit(_take)/gather | solution.py:103
  549.5 1.6 bitcast_select_fusion
  (54 shorter events, 10.2 us)
Async XLA Ops:
  7.2 20.8 %copy-start = (f32[1,2,8]{2,1,0:T(2,128)S(1)}, f32[1,2,8]{2,1,0:T(2,128)}, u32[]{:S(2)}) copy-start(f32[1,2,8]{2,1,0:T(2,128)} %param.26) | copy-start | bytes 196
  7.2 4.7 copy-start.2
  7.2 5.3 copy-start.3
  7.2 39.2 %all-gather.7.cloned.1.call-start = ((), (), s32[]{:S(2)}) async-start(), calls=%async_computation.1 | async-start | bytes 2359296 | tf_op jit(solution)/shard_map/all_gather | solution.py:57
  9.2 72.9 %all-gather.5.cloned.1.call-start = ((), (), s32[]{:S(2)}) async-start(), calls=%async_computation | async-start | bytes 2359296 | tf_op jit(solution)/shard_map/all_gather | solution.py:56
  11.0 378.6 %all-reduce.2.cloned.1.call-start = ((), (), s32[]{:S(2)}) async-start(), calls=%async_computation.2 | async-start | bytes 7340032 | tf_op jit(solution)/shard_map/psum | solution.py:92
  12.5 1.3 copy-start.4
  25.7 2.1 copy-start.8
  25.7 2.2 copy-start.9
  25.7 2.4 copy-start.7
  25.7 2.6 copy-start.5
  88.1 3.8 copy-start.1
  100.0 0.9 copy-start.6
  100.0 435.7 %all-gather.9.cloned.1.call-start = ((), (), s32[]{:S(2)}) async-start(), calls=%async_computation.3 | async-start | bytes 4259840 | tf_op jit(solution)/shard_map/all_gather | solution.py:102
  104.6 285.0 %copy-start.10 = (s32[56]{0:T(128)S(1)}, s32[56]{0:T(128)}, u32[]{:S(2)}) copy-start(s32[56]{0:T(128)} %param.23) | copy-start | bytes 676
Sparse Core Ops, SparseCore 0:
  10.2 36.2 all-gather.6
  48.6 33.4 all-gather.4
  100.2 289.4 all-reduce.1
  394.2 141.4 all-gather.8
where the time goes:
time: 558 us
  waiting for transfers between devices  475 us (85%)
  local copies, waits for them, and re-layouts  47.9 us (9%)
  matrix products  14 us (3%)
  between operations  14 us (3%)
  other arithmetic  6.76 us (1%)
    psum x1, waiting for transfers between devices, body(): summed = lax.psum(partial_value, 'dp')  284 us
    all_gather x1, waiting for transfers between devices, body(): everyone = lax.all_gather(slot_update, 'dp', axis=0, tiled=True)  142 us
    all_gather x1, waiting for transfers between devices, body(): lax.all_gather(layer_input, 'tensor', axis=1, tiled=True)  32.4 us
    unnamed x34, local copies, waits for them, and re-layouts  19.6 us
    all_gather x1, waiting for transfers between devices, body(): lax.all_gather(output_grad, 'tensor', axis=1, tiled=True)  16.4 us
    gather x5, local copies, waits for them, and re-layouts, blocks(): return jnp.take(source.reshape(tokens_here, -1, TB), block_index, axis=1)  12.1 us
  transfers between devices with their start and end apart: 4, of which 4 were waited for; matrix products, arithmetic and copies ran while one was open for 5% of the time, Pallas kernels for 0%

commit v1 on v0

--- a/solution.py
+++ b/solution.py
@@ -99,7 +99,9 @@
     first_hat = first_moment / (1.0 - BETA_FIRST**STEP)
     second_hat = second_moment / (1.0 - BETA_SECOND**STEP)
     slot_update = (first_hat / (jnp.sqrt(second_hat) + EPSILON)).astype(jnp.bfloat16)
-    everyone = lax.all_gather(slot_update, "dp", axis=0, tiled=True)
+    everyone = jnp.concatenate(
+        lax.all_to_all(jnp.stack([slot_update] * lax.axis_size("dp")), "dp", 0, 0), axis=0
+    )
     picked = jnp.take(everyone, tile_slots, axis=0)
     return (picked.reshape(tile_count, TB, TB), first_moment[None], second_moment[None])
 

time: 558 us -> 614 us (1.10)
  waiting for transfers between devices: 475 us -> 514 us
  starting transfers between devices: 0.34 us -> 10.1 us
  local copies, waits for them, and re-layouts: 47.9 us -> 54.2 us
    all_to_all x0 -> x1, waiting for transfers between devices: none -> 181 us  [body(): lax.all_to_all(jnp.stack([slot_update] * lax.axis_size('dp')), 'dp', 0, 0)]
    all_gather x1 -> x0, waiting for transfers between devices: 142 us -> none  [body(): everyone = lax.all_gather(slot_update, 'dp', axis=0, tiled=True)]
    all_to_all x0 -> x1, starting transfers between devices: none -> 9.98 us  [body(): lax.all_to_all(jnp.stack([slot_update] * lax.axis_size('dp')), 'dp', 0, 0)]
    reshape x0 -> x1, local copies, waits for them, and re-layouts: none -> 7.26 us  [body(): jnp.concatenate(lax.all_to_all(jnp.stack([slot_update] * lax.axis_size('d...]
    unnamed x34 -> x33, local copies, waits for them, and re-layouts: 19.6 us -> 12.6 us
where the time goes in v1:
time: 614 us; the launch traced here: 613 us
  waiting for transfers between devices  514 us (84%)
  local copies, waits for them, and re-layouts  54.2 us (9%)
  matrix products  14.2 us (2%)
  between operations  14 us (2%)
  starting transfers between devices  10.1 us (2%)
  other arithmetic  6.76 us (1%)
    psum x1, waiting for transfers between devices, body(): summed = lax.psum(partial_value, 'dp')  284 us
    all_to_all x1, waiting for transfers between devices, body(): lax.all_to_all(jnp.stack([slot_update] * lax.axis_size('dp')), 'dp', 0, 0)  181 us
    all_gather x1, waiting for transfers between devices, body(): lax.all_gather(layer_input, 'tensor', axis=1, tiled=True)  32.4 us
    all_gather x1, waiting for transfers between devices, body(): lax.all_gather(output_grad, 'tensor', axis=1, tiled=True)  16.4 us
    unnamed x33, local copies, waits for them, and re-layouts  12.6 us
  transfers between devices with their start and end apart: 4, of which 4 were waited for; matrix products, arithmetic and copies ran while one was open for 5% of the time, Pallas kernels for 0%

profile of v1, /device:TPU:2, one launch (start us, length us, event | category | flops | bytes accessed | tf_op | source)
XLA Modules:
  0.0 613.2 jit_solution(17938761340227788819)
XLA Ops:
  7.2 1.9 copy.31
  9.2 1.8 copy.26
  13.8 1.3 copy.28
  15.1 3.5 fusion.6
  19.3 1.6 copy.29
  20.9 2.1 gather_fusion.1
  23.0 2.0 gather_fusion.3
  25.7 2.1 gather_fusion.4
  30.0 16.4 %all-gather.5.cloned.1.call-done = bf16[128,8192]{0,1:T(8,128)(2,1)} async-done(((bf16[128,1024]{0,1:T(8,128)(2,1)}), bf16[128,8192]{0,1:T(8,128)(2,1)}) %all-gather.5.cloned.1.call-update) | async-done | bytes 2097168 | tf_op jit(solution)/shard_map/all_gather | solution.py:57
  46.4 3.2 copy.32
  49.7 32.4 %all-gather.3.cloned.1.call-done = bf16[128,8192]{0,1:T(8,128)(2,1)} async-done(((bf16[128,1024]{0,1:T(8,128)(2,1)}), bf16[128,8192]{0,1:T(8,128)(2,1)}) %all-gather.3.cloned.1.call-update) | async-done | bytes 2097168 | tf_op jit(solution)/shard_map/all_gather | solution.py:56
  82.0 4.1 copy.27
  86.1 2.0 gather_fusion.5
  88.1 3.8 gather_fusion.2
  91.9 4.4 fusion.16
  96.3 3.9 copy.40
  105.7 284.1 %all-reduce.2.cloned.1.call-done = f32[56,16384]{1,0:T(8,128)} async-done(((f32[56,16384]{1,0:T(8,128)}), f32[56,16384]{1,0:T(8,128)}) %all-reduce.2.cloned.1.call-update) | async-done | bytes 3670032 | tf_op jit(solution)/shard_map/psum | solution.py:92
  389.7 4.4 fusion.45
  394.2 6.0 stack.2
  400.2 10.0 %all-to-all-start = ((bf16[64,2,16384]{2,1,0:T(2,128)(2,1)}), bf16[64,2,16384]{2,1,0:T(2,128)(2,1)}, u32[]{:S(2)}, u32[]{:S(2)}) async-start(bf16[64,2,16384]{2,1,0:T(2,128)(2,1)} %stack.2), calls=%async_computation | async-start | bytes 8388608 | tf_op jit(solution)/shard_map/all_to_all | solution.py:103
  410.2 181.1 %all-to-all-done = bf16[64,2,16384]{2,1,0:T(2,128)(2,1)} async-done(((bf16[64,2,16384]{2,1,0:T(2,128)(2,1)}), bf16[64,2,16384]{2,1,0:T(2,128)(2,1)}, u32[]{:S(2)}, u32[]{:S(2)}) %all-to-all-start) | async-done | bytes 4194336 | tf_op jit(solution)/shard_map/all_to_all | solution.py:103
  591.3 7.3 %reshape.139 = bf16[128,16384]{1,0:T(8,128)(2,1)} reshape(bf16[64,2,16384]{2,1,0:T(2,128)(2,1)} %all-to-all-done) | data formatting | bytes 8388608 | tf_op jit(solution)/shard_map/reshape | solution.py:102
  598.6 6.0 gather_fusion
  605.1 1.6 bitcast_select_fusion
  (54 shorter events, 12.3 us)
Async XLA Ops:
  7.2 20.7 %copy-start = (f32[1,2,8]{2,1,0:T(2,128)S(1)}, f32[1,2,8]{2,1,0:T(2,128)}, u32[]{:S(2)}) copy-start(f32[1,2,8]{2,1,0:T(2,128)} %param.26) | copy-start | bytes 196
  7.2 4.7 copy-start.2
  7.2 5.3 copy-start.3
  7.2 39.2 %all-gather.5.cloned.1.call-start = ((), (), s32[]{:S(2)}) async-start(), calls=%async_computation.2 | async-start | bytes 2359296 | tf_op jit(solution)/shard_map/all_gather | solution.py:57
  9.2 72.9 %all-gather.3.cloned.1.call-start = ((), (), s32[]{:S(2)}) async-start(), calls=%async_computation.1 | async-start | bytes 2359296 | tf_op jit(solution)/shard_map/all_gather | solution.py:56
  11.1 378.7 %all-reduce.2.cloned.1.call-start = ((), (), s32[]{:S(2)}) async-start(), calls=%async_computation.3 | async-start | bytes 7340032 | tf_op jit(solution)/shard_map/psum | solution.py:92
  12.5 1.3 copy-start.4
  25.6 2.1 copy-start.8
  25.6 2.2 copy-start.9
  25.7 2.4 copy-start.7
  25.7 2.6 copy-start.5
  88.1 3.8 copy-start.1
  100.2 0.9 copy-start.6
  104.8 285.0 %copy-start.10 = (s32[56]{0:T(128)S(1)}, s32[56]{0:T(128)}, u32[]{:S(2)}) copy-start(s32[56]{0:T(128)} %param.23) | copy-start | bytes 676
  400.2 191.1 %all-to-all-start = ((bf16[64,2,16384]{2,1,0:T(2,128)(2,1)}), bf16[64,2,16384]{2,1,0:T(2,128)(2,1)}, u32[]{:S(2)}, u32[]{:S(2)}) async-start(bf16[64,2,16384]{2,1,0:T(2,128)(2,1)} %stack.2), calls=%async_computation | async-start | bytes 8388608 | tf_op jit(solution)/shard_map/all_to_all | solution.py:103
Sparse Core Ops, SparseCore 0:
  10.2 36.2 all-gather.4
  48.6 33.4 all-gather.2
  100.3 289.3 all-reduce.1
